TPU v7x, 256 devices: a 8x8x2 block of a 8x8x16 slice. The times are simulated.
256 devices in a mesh: grp: 2 (over z), row: 16 (over x, core), sub: 8 (over y).
Axes of the slice: x: 8, y: 8, z: 2, core: 2. Of those that a mesh axis runs over, the one named last changes fastest.
The devices are a block of a 8x8x16 slice.
Arguments:
- residual_in: float32 [4, 2048, 2048], P('grp', ('row', 'sub')), parts along dimension 0, may hold values from -100 to 100
- direction: float32 [4, 2048, 2048], P('grp', ('row', 'sub')), parts along dimension 0, may hold values from -100 to 100
- spectrum: float32 [8192, 4096], P('grp', ('row', 'sub')), parts along dimension 0, may hold values from 0.0999 to 10.001, as said below
- noise_var: float32 [2], P('grp'), parts along dimension 0, may hold values from 0.5 to 2
Outputs:
- residual_out: float32 [4, 2048, 2048], P('grp', ('row', 'sub')), parts along dimension 0
- direction_out: float32 [4, 2048, 2048], P('grp', ('row', 'sub')), parts along dimension 0
- step_size: float32 [4], P('grp'), parts along dimension 0
There are 2 independent parts, one for each index of `grp`. A program takes and returns all parts, laid end to end along the dimension named above; each array names one. Nothing has to cross between parts.
Inputs may be any that keep to these rules, and one draw needn't show every extreme that they name: spectrum[k, l] = spectrum[(4096 - k) % 4096, (4096 - l) % 4096] for all k, l.
All inputs are finite; a program needn't handle non-finite values.
Results may differ from a plain program's by a relative error of at most 0.00005.
Values sent between devices are 32-bit elements; how exact they have to be, the bound alone decides.
A program may use at most 64 MiB of HBM per device.

v0:
```python
import functools
import math
import jax
import jax.numpy as jnp
from jax import lax
from jax.sharding import Mesh
from jax.sharding import PartitionSpec as P

ROW = ("row_0", "row_1")
ROW_SUB = ("row_0", "row_1", "sub")
high_factor = 128
tiny_value = 1e-06


def split_up(value, dim, count):
    dims = value.shape
    parts = value.reshape(*dims[:dim], count, dims[dim] // count, *dims[dim + 1 :])
    return jnp.moveaxis(parts, dim, 0)


def edges_of(length, count):
    hop = length // count
    if hop >= 8:
        hop -= hop % 8
    return [hop * k for k in range(1, count)]


def laid_out(parts, dim):
    dims = list(parts.shape[1:])
    dims[dim] *= parts.shape[0]
    return jnp.moveaxis(parts, 0, dim).reshape(dims)


def exchange_in_pieces(value, axis, pieces, split_dim, concat_dim):
    parts = split_up(value, split_dim, lax.axis_size(axis))
    cut = max(range(1, max(2, parts.ndim - 1)), key=lambda d: parts.shape[d])
    finished = []
    for share in jnp.split(parts, edges_of(parts.shape[cut], pieces), axis=cut):
        if share.size:
            finished.append(lax.all_to_all(share, axis, split_axis=0, concat_axis=0, tiled=True))
    return laid_out(jnp.concatenate(finished, axis=cut), concat_dim)


def over_axes(value, axes):
    return functools.reduce(lax.psum, axes, value)


def phase_pair(left_ids, right_ids, modulus, orient):
    turns = left_ids * right_ids % modulus
    angle = orient * 2.0 * math.pi / modulus * turns.astype(jnp.float32)
    return (jnp.cos(angle), jnp.sin(angle))


def complex_table(cos_part, sin_part):
    upper_rows = jnp.stack([cos_part, sin_part], axis=1)
    lower_rows = jnp.stack([-sin_part, cos_part], axis=1)
    return jnp.stack([upper_rows, lower_rows], axis=1)


def rotate(values, cos_part, sin_part, at_axis):
    real_part = lax.index_in_dim(values, 0, at_axis, keepdims=False)
    imag_part = lax.index_in_dim(values, 1, at_axis, keepdims=False)
    return jnp.stack(
        [real_part * cos_part - imag_part * sin_part, real_part * sin_part + imag_part * cos_part],
        axis=at_axis,
    )


def contract(form_spec, operand, table_arr):
    return jnp.einsum(form_spec, operand, table_arr, precision=lax.Precision.HIGHEST)


def body(residual_in, direction, spectrum, noise_var):
    probes, rows_dev, grid_len = direction.shape
    embed_len = 2 * grid_len
    low_factor = embed_len // high_factor
    half_factor = grid_len // high_factor
    n_row = lax.axis_size(ROW)
    n_sub = lax.axis_size("sub")
    devices = n_row * n_sub
    per_device = high_factor // devices
    slot_ids = jnp.arange(high_factor, dtype=jnp.int32)
    first_ids = jnp.arange(half_factor, dtype=jnp.int32)
    second_ids = jnp.arange(low_factor, dtype=jnp.int32)
    short_cos, short_sin = phase_pair(first_ids[:, None], second_ids[None, :], low_factor, -1.0)
    turn_cos, turn_sin = phase_pair(slot_ids[:, None], second_ids[None, :], embed_len, -1.0)
    long_cos, long_sin = phase_pair(slot_ids[:, None], slot_ids[None, :], high_factor, -1.0)
    plain_cos, plain_sin = phase_pair(slot_ids[:, None], slot_ids[None, :], high_factor, -1.0)
    back_cos, back_sin = phase_pair(slot_ids[:, None], slot_ids[None, :], high_factor, 1.0)
    perm_cos, perm_sin = phase_pair(slot_ids[:, None], slot_ids[None, :], high_factor, 1.0)
    last_cos, last_sin = phase_pair(second_ids[:, None], first_ids[None, :], low_factor, 1.0)
    fields = direction.reshape(probes // 2, 2, rows_dev, half_factor, high_factor)
    spread = contract("ycrab,acdm->yrbdm", fields, complex_table(short_cos, short_sin))
    batches = spread.shape[0]
    spread = rotate(spread, turn_cos, turn_sin, 3)
    row_freq = contract("frbcm,bcdk->frkdm", spread, complex_table(long_cos, long_sin))
    row_freq = row_freq.reshape(batches, rows_dev, 2 * embed_len)
    columns = exchange_in_pieces(row_freq, ROW_SUB, 2, 2, 1)
    columns = columns.reshape(batches, half_factor, high_factor, per_device, 2, low_factor)
    turned = contract("fabqcm,acdj->fjbqdm", columns, complex_table(short_cos, short_sin))
    turned = rotate(turned, turn_cos.T[:, :, None, None], turn_sin.T[:, :, None, None], 4)
    spectra = contract("fjbqcm,bcdk->fkjqdm", turned, complex_table(plain_cos, plain_sin))
    weights = (spectrum * (1.0 / (embed_len * embed_len))).reshape(
        high_factor, low_factor, per_device, low_factor
    )
    spectra = spectra * weights[None, :, :, :, None, :]
    inverted = contract("fkjqcm,kcdb->fbjqdm", spectra, complex_table(back_cos, back_sin))
    inverted = rotate(inverted, turn_cos[:, :, None, None], -turn_sin[:, :, None, None], 4)
    grid_cols = contract("fbjqcm,jcda->fabqdm", inverted, complex_table(last_cos, last_sin))
    grid_cols = grid_cols.reshape(batches, grid_len, 2 * embed_len // devices)
    rows_back = lax.all_to_all(grid_cols, ROW_SUB, split_axis=1, concat_axis=2, tiled=True)
    rows_back = rows_back.reshape(batches, rows_dev, high_factor, 2, low_factor)
    mixed = contract("frkcm,kcdb->frbdm", rows_back, complex_table(perm_cos, perm_sin))
    mixed = rotate(mixed, turn_cos, -turn_sin, 3)
    applied = contract("frbcm,mcda->fdrab", mixed, complex_table(last_cos, last_sin))
    applied = applied.reshape(probes, rows_dev, grid_len)
    image_out = applied + noise_var[0] * direction
    own_curv = jnp.sum(direction * image_out, axis=(1, 2))
    own_norm = jnp.sum(residual_in * residual_in, axis=(1, 2))
    old_norm, curvature = (over_axes(own_norm, ROW_SUB), over_axes(own_curv, ROW_SUB))
    step_size = old_norm / curvature
    residual_out = residual_in - step_size[:, None, None] * image_out
    new_norm = over_axes(jnp.sum(residual_out * residual_out, axis=(1, 2)), ROW_SUB)
    direction_out = residual_out + (new_norm / (old_norm + tiny_value))[:, None, None] * direction
    return (residual_out, direction_out, step_size)


def solution(mesh):
    torus = Mesh(
        mesh.devices.reshape(mesh.shape["grp"], 8, 2, mesh.shape["sub"]),
        ("grp", "row_0", "row_1", "sub"),
    )
    in_specs = (P("grp", ROW_SUB, None), P("grp", ROW_SUB, None), P("grp", ROW_SUB), P("grp"))
    out_specs = (P("grp", ROW_SUB, None), P("grp", ROW_SUB, None), P("grp"))
    return jax.shard_map(body, mesh=torus, in_specs=in_specs, out_specs=out_specs, check_vma=False)
```

profile of v0, /device:TPU:514, one launch (start us, length us, event | category | flops | bytes accessed | tf_op | source)
XLA Modules:
  0.0 187.7 jit_solution(11520293836639985032)
XLA Ops:
  4.1 1.0 reshape.538
  5.2 26.7 %all-to-all-start.1 = ((f32[128,1,512]{2,1,0:T(1,128)}), f32[128,1,512]{2,1,0:T(1,128)S(1)}, u32[]{:S(2)}, u32[]{:S(2)}) async-start(f32[128,1,512]{2,1,0:T(1,128)} %reshape.538), calls=%async_computation.1 | async-start | bytes 524288 | tf_op jit(solution)/shard_map/all_to_all | solution.py:40
  32.2 1.0 reshape.540
  33.9 1.5 copy.47
  36.8 8.1 %all-to-all-done.1 = f32[128,1,512]{2,1,0:T(1,128)S(1)} async-done(((f32[128,1,512]{2,1,0:T(1,128)}), f32[128,1,512]{2,1,0:T(1,128)S(1)}, u32[]{:S(2)}, u32[]{:S(2)}) %all-to-all-start.1) | async-done | bytes 262176 | tf_op jit(solution)/shard_map/all_to_all | solution.py:40
  44.9 8.5 %all-to-all-start = ((f32[128,1,512]{2,1,0:T(1,128)}), f32[128,1,512]{2,1,0:T(1,128)S(1)}, u32[]{:S(2)}, u32[]{:S(2)}) async-start(f32[128,1,512]{2,1,0:T(1,128)} %reshape.540), calls=%async_computation | async-start | bytes 524288 | tf_op jit(solution)/shard_map/all_to_all | solution.py:40
  55.8 1.3 reduce
  57.2 9.2 %all-to-all-done = f32[128,1,512]{2,1,0:T(1,128)S(1)} async-done(((f32[128,1,512]{2,1,0:T(1,128)}), f32[128,1,512]{2,1,0:T(1,128)S(1)}, u32[]{:S(2)}, u32[]{:S(2)}) %all-to-all-start) | async-done | bytes 262176 | tf_op jit(solution)/shard_map/all_to_all | solution.py:40
  66.5 1.3 reduce.1
  68.0 1.2 reshape.509
  72.1 1.7 fusion.1
  75.6 1.2 convolution_bitcast_fusion.6
  77.6 9.6 %reduce.2 = f32[2048,64]{1,0:T(8,128)S(1)} reduce(f32[2048,1,64]{2,1,0:T(1,128)S(1)} %bitcast.174, f32[]{:T(128)} %broadcast.730), dimensions={1}, to_apply=%bitcast.155.reduce_sub_computation | reduce | bytes 1048580
  87.2 1.4 reshape.542
  88.6 8.4 %all-to-all-start.2 = ((f32[128,1,1024]{2,1,0:T(1,128)}), f32[128,1,1024]{2,1,0:T(1,128)S(1)}, u32[]{:S(2)}, u32[]{:S(2)}) async-start(f32[128,1,1024]{2,1,0:T(1,128)} %reshape.542), calls=%async_computation.2 | async-start | bytes 1048576 | tf_op jit(solution)/shard_map/all_to_all | solution.py:111
  97.8 17.1 %all-to-all-done.2 = f32[128,1,1024]{2,1,0:T(1,128)S(1)} async-done(((f32[128,1,1024]{2,1,0:T(1,128)}), f32[128,1,1024]{2,1,0:T(1,128)S(1)}, u32[]{:S(2)}, u32[]{:S(2)}) %all-to-all-start.2) | async-done | bytes 524320 | tf_op jit(solution)/shard_map/all_to_all | solution.py:111
  114.9 1.9 %reduce.3 = f32[128,1024]{1,0:T(8,128)S(1)} reduce(f32[128,1,1024]{2,1,0:T(1,128)S(1)} %all-to-all-done.2, f32[]{:T(128)} %broadcast.730), dimensions={1}, to_apply=%all_to_all.19.reduce_sub_computation | reduce | bytes 1048580 | tf_op jit(solution)/shard_map/all_to_all | solution.py:111
  116.8 1.3 reshape.543
  119.9 15.7 %all-reduce.1 = (f32[2]{0:T(128)S(1)}, f32[2]{0:T(128)S(1)}) all-reduce(f32[2]{0:T(128)S(1)} %multiply_reduce_fusion.2, f32[2]{0:T(128)S(1)} %multiply_reduce_fusion.1), channel_id=1, replica_groups=mesh['grp'=2,'row_0'=8,'row_1'=2,'sub'=8] {'row_0'}, use_global_device_ids=true, to_apply=%region_1.2 | all-reduce | flops 4 | bytes 32 | tf_op jit(solution)/shard_map/psum | solution.py:45
  135.6 2.5 %all-reduce.2 = (f32[2]{0:T(128)S(1)}, f32[2]{0:T(128)S(1)}) all-reduce(f32[2]{0:T(128)S(1)} %get-tuple-element.5, f32[2]{0:T(128)S(1)} %get-tuple-element.6), channel_id=1, replica_groups=mesh['grp'=2,'row_0'=8,'row_1'=2,'sub'=8] {'row_1'}, use_global_device_ids=true, to_apply=%region_2.3 | all-reduce | flops 4 | bytes 32 | tf_op jit(solution)/shard_map/psum | solution.py:45
  138.1 16.5 %all-reduce = (f32[2]{0:T(128)S(1)}, f32[2]{0:T(128)S(1)}) all-reduce(f32[2]{0:T(128)S(1)} %get-tuple-element.7, f32[2]{0:T(128)S(1)} %get-tuple-element.8), channel_id=1, replica_groups=mesh['grp'=2,'row_0'=8,'row_1'=2,'sub'=8] {'sub'}, use_global_device_ids=true, to_apply=%region_3.4 | all-reduce | flops 4 | bytes 32 | tf_op jit(solution)/shard_map/psum | solution.py:45
  154.9 15.3 %psum.69 = f32[2]{0:T(128)S(1)} all-reduce(f32[2]{0:T(128)S(1)} %get-tuple-element.9), channel_id=1, replica_groups=mesh['grp'=2,'row_0'=8,'row_1'=2,'sub'=8] {'row_0'}, use_global_device_ids=true, to_apply=%region_9.10 | all-reduce | flops 2 | bytes 16 | tf_op jit(solution)/shard_map/psum | solution.py:45
  170.2 2.5 %psum.70 = f32[2]{0:T(128)S(1)} all-reduce(f32[2]{0:T(128)S(1)} %psum.69), channel_id=1, replica_groups=mesh['grp'=2,'row_0'=8,'row_1'=2,'sub'=8] {'row_1'}, use_global_device_ids=true, to_apply=%region_10.11 | all-reduce | flops 2 | bytes 16 | tf_op jit(solution)/shard_map/psum | solution.py:45
  172.7 14.2 %psum.71 = f32[2]{0:T(128)S(1)} all-reduce(f32[2]{0:T(128)S(1)} %psum.70), channel_id=1, replica_groups=mesh['grp'=2,'row_0'=8,'row_1'=2,'sub'=8] {'sub'}, use_global_device_ids=true, to_apply=%region_11.12 | all-reduce | flops 2 | bytes 16 | tf_op jit(solution)/shard_map/psum | solution.py:45
  (81 shorter events, 16.7 us)
Async XLA Ops:
  2.4 0.7 copy-start.9
  2.4 0.7 copy-start.11
  3.8 28.1 %copy-start.5 = (f32[4096,32]{0,1:T(8,128)S(1)}, f32[4096,32]{0,1:T(8,128)}, u32[]{:S(2)}) copy-start(f32[4096,32]{0,1:T(8,128)} %param.6) | copy-start | bytes 1572868
  5.2 39.7 %all-to-all-start.1 = ((f32[128,1,512]{2,1,0:T(1,128)}), f32[128,1,512]{2,1,0:T(1,128)S(1)}, u32[]{:S(2)}, u32[]{:S(2)}) async-start(f32[128,1,512]{2,1,0:T(1,128)} %reshape.538), calls=%async_computation.1 | async-start | bytes 524288 | tf_op jit(solution)/shard_map/all_to_all | solution.py:40
  44.9 21.6 %all-to-all-start = ((f32[128,1,512]{2,1,0:T(1,128)}), f32[128,1,512]{2,1,0:T(1,128)S(1)}, u32[]{:S(2)}, u32[]{:S(2)}) async-start(f32[128,1,512]{2,1,0:T(1,128)} %reshape.540), calls=%async_computation | async-start | bytes 524288 | tf_op jit(solution)/shard_map/all_to_all | solution.py:40
  69.1 0.9 copy-start.10
  69.1 0.9 copy-start.12
  69.1 1.9 %copy-start.13 = (f32[32,128]{1,0:T(8,128)S(1)}, f32[32,128]{1,0:T(8,128)}, u32[]{:S(2)}) copy-start(f32[32,128]{1,0:T(8,128)} %get-tuple-element.35) | copy-start | bytes 49156
  69.2 1.9 %copy-start.14 = (f32[32,128]{1,0:T(8,128)S(1)}, f32[32,128]{1,0:T(8,128)}, u32[]{:S(2)}) copy-start(f32[32,128]{1,0:T(8,128)} %get-tuple-element.36) | copy-start | bytes 49156
  71.1 1.0 copy-start.1
  71.3 2.6 %copy-start.2 = (f32[128,1,2,128]{3,0,2,1:T(8,128)S(1)}, f32[128,1,2,128]{3,0,2,1:T(8,128)}, u32[]{:S(2)}) copy-start(f32[128,1,2,128]{3,0,2,1:T(8,128)} %get-tuple-element.22) | copy-start | bytes 393220
  72.1 2.7 %copy-start.6 = (f32[128,32]{0,1:T(8,128)S(1)}, f32[128,32]{0,1:T(8,128)}, u32[]{:S(2)}) copy-start(f32[128,32]{0,1:T(8,128)} %fusion.52) | copy-start | bytes 49156
  74.9 0.7 copy-start.7
  74.9 0.7 copy-start.8
  77.5 20.1 %copy-start.3 = (f32[2,16,2048]{2,1,0:T(8,128)S(1)}, f32[2,16,2048]{2,1,0:T(8,128)}, u32[]{:S(2)}) copy-start(f32[2,16,2048]{2,1,0:T(8,128)} %param.4) | copy-start | bytes 786436
  88.6 26.3 %all-to-all-start.2 = ((f32[128,1,1024]{2,1,0:T(1,128)}), f32[128,1,1024]{2,1,0:T(1,128)S(1)}, u32[]{:S(2)}, u32[]{:S(2)}) async-start(f32[128,1,1024]{2,1,0:T(1,128)} %reshape.542), calls=%async_computation.2 | async-start | bytes 1048576 | tf_op jit(solution)/shard_map/all_to_all | solution.py:111
  118.6 1.2 copy-start
  154.7 33.0 %copy-start.15 = (f32[2]{0:T(128)}, f32[2]{0:T(128)S(1)}, u32[]{:S(2)}) copy-start(f32[2]{0:T(128)S(1)} %div.6) | copy-start | bytes 28
  154.9 32.8 %copy-start.4 = (f32[2,16,2048]{2,1,0:T(8,128)}, f32[2,16,2048]{2,1,0:T(8,128)S(1)}, u32[]{:S(2)}) copy-start(f32[2,16,2048]{2,1,0:T(8,128)S(1)} %get-tuple-element.10) | copy-start | bytes 786436
where the time goes:
time: 188 us
  blocking collectives  66.8 us (36%)
  starting transfers between devices  43.6 us (23%)
  waiting for transfers between devices  34.5 us (18%)
  other arithmetic  20.1 us (11%)
  local copies, waits for them, and re-layouts  13.8 us (7%)
  matrix products  7.18 us (4%)
    psum x6, blocking collectives, over_axes(): return functools.reduce(lax.psum, axes, value)  66.8 us
    all_to_all x2, starting transfers between devices, exchange_in_pieces(): lax.all_to_all(share, axis, split_axis=0, concat_axis=0, tiled=True)  35.2 us
    all_to_all x2, waiting for transfers between devices, exchange_in_pieces(): lax.all_to_all(share, axis, split_axis=0, concat_axis=0, tiled=True)  17.3 us
    all_to_all x1, waiting for transfers between devices, body(): lax.all_to_all(grid_cols, ROW_SUB, split_axis=1, concat_axis=2, tiled=True)  17.1 us
    unnamed x1, other arithmetic  9.61 us
    all_to_all x1, starting transfers between devices, body(): lax.all_to_all(grid_cols, ROW_SUB, split_axis=1, concat_axis=2, tiled=True)  8.38 us
    unnamed x39, local copies, waits for them, and re-layouts  7.4 us
    dot_general x8, matrix products, contract(): jnp.einsum(form_spec, operand, table_arr, precision=lax.Precision.HIGHEST)  7.18 us
  transfers between devices with their start and end apart: 3, of which 3 were waited for; matrix products, arithmetic and copies ran while one was open for 5% of the time, Pallas kernels for 0%

commit v1 on v0

--- a/solution.py
+++ b/solution.py
@@ -108,7 +108,12 @@
     inverted = rotate(inverted, turn_cos[:, :, None, None], -turn_sin[:, :, None, None], 4)
     grid_cols = contract("fbjqcm,jcda->fabqdm", inverted, complex_table(last_cos, last_sin))
     grid_cols = grid_cols.reshape(batches, grid_len, 2 * embed_len // devices)
-    rows_back = lax.all_to_all(grid_cols, ROW_SUB, split_axis=1, concat_axis=2, tiled=True)
+    rows_back = jnp.concatenate(
+        lax.all_to_all(
+            jnp.stack(jnp.split(grid_cols, lax.axis_size(ROW_SUB), axis=1)), ROW_SUB, 0, 0
+        ),
+        axis=2,
+    )
     rows_back = rows_back.reshape(batches, rows_dev, high_factor, 2, low_factor)
     mixed = contract("frkcm,kcdb->frbdm", rows_back, complex_table(perm_cos, perm_sin))
     mixed = rotate(mixed, turn_cos, -turn_sin, 3)

time: 188 us -> 294 us (1.56); the launches traced: 188 us -> 288 us
  local copies, waits for them, and re-layouts: 13.8 us -> 122 us
  other arithmetic: 20.1 us -> 9.86 us
    unnamed x39 -> x376, local copies, waits for them, and re-layouts: 7.4 us -> 112 us
    unnamed x1 -> x0, other arithmetic: 9.61 us -> none
    split x0 -> x7, local copies, waits for them, and re-layouts: none -> 4.47 us  [body(): jnp.split(grid_cols, lax.axis_size(ROW_SUB), axis=1)]
  transfers between devices with their start and end apart: 3 -> 3, of which waited for: 3 -> 3; matrix products, arithmetic and copies ran while one was open for 5% -> 3% of each run, Pallas kernels for 0% -> 0%
where the time goes in v1:
time: 294 us; the launch traced here: 288 us
  local copies, waits for them, and re-layouts  122 us (41%)
  blocking collectives  66.8 us (23%)
  starting transfers between devices  43.6 us (15%)
  waiting for transfers between devices  35.1 us (12%)
  other arithmetic  9.86 us (3%)
  matrix products  7.18 us (2%)
  between operations  3.38 us (1%)
    unnamed x376, local copies, waits for them, and re-layouts  112 us
    psum x6, blocking collectives, over_axes(): return functools.reduce(lax.psum, axes, value)  66.8 us
    all_to_all x2, starting transfers between devices, exchange_in_pieces(): lax.all_to_all(share, axis, split_axis=0, concat_axis=0, tiled=True)  35.2 us
    all_to_all x2, waiting for transfers between devices, exchange_in_pieces(): lax.all_to_all(share, axis, split_axis=0, concat_axis=0, tiled=True)  18 us
    all_to_all x1, waiting for transfers between devices, body(): lax.all_to_all(jnp.stack(jnp.split(grid_cols, lax.axis_size(ROW_SUB), axi...  17.1 us
    all_to_all x1, starting transfers between devices, body(): lax.all_to_all(jnp.stack(jnp.split(grid_cols, lax.axis_size(ROW_SUB), axi...  8.35 us
    dot_general x8, matrix products, contract(): jnp.einsum(form_spec, operand, table_arr, precision=lax.Precision.HIGHEST)  7.18 us
  transfers between devices with their start and end apart: 3, of which 3 were waited for; matrix products, arithmetic and copies ran while one was open for 3% of the time, Pallas kernels for 0%

profile of v1, /device:TPU:514, one launch (start us, length us, event | category | flops | bytes accessed | tf_op | source)
XLA Modules:
  0.0 288.1 jit_solution(4940952107176007568)
XLA Ops:
  5.8 26.7 %all-to-all-start.1 = ((f32[128,1,512]{2,1,0:T(1,128)}), f32[128,1,512]{2,1,0:T(1,128)S(1)}, u32[]{:S(2)}, u32[]{:S(2)}) async-start(f32[128,1,512]{2,1,0:T(1,128)} %reshape.540), calls=%async_computation.1 | async-start | bytes 524288 | tf_op jit(solution)/shard_map/all_to_all | solution.py:40
  34.5 1.5 copy.466
  37.4 8.1 %all-to-all-done.1 = f32[128,1,512]{2,1,0:T(1,128)S(1)} async-done(((f32[128,1,512]{2,1,0:T(1,128)}), f32[128,1,512]{2,1,0:T(1,128)S(1)}, u32[]{:S(2)}, u32[]{:S(2)}) %all-to-all-start.1) | async-done | bytes 262176 | tf_op jit(solution)/shard_map/all_to_all | solution.py:40
  45.5 8.5 %all-to-all-start = ((f32[128,1,512]{2,1,0:T(1,128)}), f32[128,1,512]{2,1,0:T(1,128)S(1)}, u32[]{:S(2)}, u32[]{:S(2)}) async-start(f32[128,1,512]{2,1,0:T(1,128)} %reshape.542), calls=%async_computation | async-start | bytes 524288 | tf_op jit(solution)/shard_map/all_to_all | solution.py:40
  57.2 9.9 %all-to-all-done = f32[128,1,512]{2,1,0:T(1,128)S(1)} async-done(((f32[128,1,512]{2,1,0:T(1,128)}), f32[128,1,512]{2,1,0:T(1,128)S(1)}, u32[]{:S(2)}, u32[]{:S(2)}) %all-to-all-start) | async-done | bytes 262176 | tf_op jit(solution)/shard_map/all_to_all | solution.py:40
  72.8 1.7 fusion.1
  82.1 1.4 copy.619
  86.4 1.4 copy.622
  99.2 1.4 copy.631
  100.6 1.4 copy.632
  107.7 1.4 copy.637
  109.2 1.4 copy.638
  129.1 1.4 copy.652
  150.4 1.4 copy.667
  188.6 1.4 reshape.544
  190.1 8.4 %all-to-all-start.2 = ((f32[128,1,1024]{2,1,0:T(1,128)}), f32[128,1,1024]{2,1,0:T(1,128)S(1)}, u32[]{:S(2)}, u32[]{:S(2)}) async-start(f32[128,1,1024]{2,1,0:T(1,128)} %reshape.544), calls=%async_computation.2 | async-start | bytes 1048576 | tf_op jit(solution)/shard_map/all_to_all | solution.py:112
  199.2 17.1 %all-to-all-done.2 = f32[128,1,1024]{2,1,0:T(1,128)S(1)} async-done(((f32[128,1,1024]{2,1,0:T(1,128)}), f32[128,1,1024]{2,1,0:T(1,128)S(1)}, u32[]{:S(2)}, u32[]{:S(2)}) %all-to-all-start.2) | async-done | bytes 524320 | tf_op jit(solution)/shard_map/all_to_all | solution.py:112
  216.4 1.9 reduce.2
  220.3 15.7 %all-reduce.1 = (f32[2]{0:T(128)S(1)}, f32[2]{0:T(128)S(1)}) all-reduce(f32[2]{0:T(128)S(1)} %multiply_reduce_fusion.2, f32[2]{0:T(128)S(1)} %multiply_reduce_fusion.1), channel_id=1, replica_groups=mesh['grp'=2,'row_0'=8,'row_1'=2,'sub'=8] {'row_0'}, use_global_device_ids=true, to_apply=%region_1.2 | all-reduce | flops 4 | bytes 32 | tf_op jit(solution)/shard_map/psum | solution.py:45
  236.0 2.5 all-reduce.2
  238.5 16.5 %all-reduce = (f32[2]{0:T(128)S(1)}, f32[2]{0:T(128)S(1)}) all-reduce(f32[2]{0:T(128)S(1)} %get-tuple-element.7, f32[2]{0:T(128)S(1)} %get-tuple-element.8), channel_id=1, replica_groups=mesh['grp'=2,'row_0'=8,'row_1'=2,'sub'=8] {'sub'}, use_global_device_ids=true, to_apply=%region_3.4 | all-reduce | flops 4 | bytes 32 | tf_op jit(solution)/shard_map/psum | solution.py:45
  255.3 15.3 %psum.69 = f32[2]{0:T(128)S(1)} all-reduce(f32[2]{0:T(128)S(1)} %get-tuple-element.9), channel_id=1, replica_groups=mesh['grp'=2,'row_0'=8,'row_1'=2,'sub'=8] {'row_0'}, use_global_device_ids=true, to_apply=%region_9.10 | all-reduce | flops 2 | bytes 16 | tf_op jit(solution)/shard_map/psum | solution.py:45
  270.6 2.5 psum.70
  273.1 14.2 %psum.71 = f32[2]{0:T(128)S(1)} all-reduce(f32[2]{0:T(128)S(1)} %psum.70), channel_id=1, replica_groups=mesh['grp'=2,'row_0'=8,'row_1'=2,'sub'=8] {'sub'}, use_global_device_ids=true, to_apply=%region_11.12 | all-reduce | flops 2 | bytes 16 | tf_op jit(solution)/shard_map/psum | solution.py:45
  (424 shorter events, 121.4 us)
Async XLA Ops:
  4.4 28.1 %copy-start.6 = (f32[4096,32]{0,1:T(8,128)S(1)}, f32[4096,32]{0,1:T(8,128)}, u32[]{:S(2)}) copy-start(f32[4096,32]{0,1:T(8,128)} %param.6) | copy-start | bytes 1572868
  5.8 39.7 %all-to-all-start.1 = ((f32[128,1,512]{2,1,0:T(1,128)}), f32[128,1,512]{2,1,0:T(1,128)S(1)}, u32[]{:S(2)}, u32[]{:S(2)}) async-start(f32[128,1,512]{2,1,0:T(1,128)} %reshape.540), calls=%async_computation.1 | async-start | bytes 524288 | tf_op jit(solution)/shard_map/all_to_all | solution.py:40
  45.5 21.6 %all-to-all-start = ((f32[128,1,512]{2,1,0:T(1,128)}), f32[128,1,512]{2,1,0:T(1,128)S(1)}, u32[]{:S(2)}, u32[]{:S(2)}) async-start(f32[128,1,512]{2,1,0:T(1,128)} %reshape.542), calls=%async_computation | async-start | bytes 524288 | tf_op jit(solution)/shard_map/all_to_all | solution.py:40
  168.3 19.5 %copy-start.18 = (f32[1,16,64]{2,1,0:T(8,128)S(1)}, f32[1,16,64]{2,1,0:T(8,128)}, u32[]{:S(2)}) copy-start(f32[1,16,64]{2,1,0:T(8,128)} %copy.676) | copy-start | bytes 12292
  168.3 19.5 %copy-start.17 = (f32[1,16,64]{2,1,0:T(8,128)S(1)}, f32[1,16,64]{2,1,0:T(8,128)}, u32[]{:S(2)}) copy-start(f32[1,16,64]{2,1,0:T(8,128)} %copy.677) | copy-start | bytes 12292
  168.3 19.5 %copy-start.16 = (f32[1,16,64]{2,1,0:T(8,128)S(1)}, f32[1,16,64]{2,1,0:T(8,128)}, u32[]{:S(2)}) copy-start(f32[1,16,64]{2,1,0:T(8,128)} %copy.678) | copy-start | bytes 12292
  168.4 19.3 %copy-start.21 = (f32[1,16,64]{2,1,0:T(8,128)S(1)}, f32[1,16,64]{2,1,0:T(8,128)}, u32[]{:S(2)}) copy-start(f32[1,16,64]{2,1,0:T(8,128)} %copy.673) | copy-start | bytes 12292
  168.4 19.4 %copy-start.20 = (f32[1,16,64]{2,1,0:T(8,128)S(1)}, f32[1,16,64]{2,1,0:T(8,128)}, u32[]{:S(2)}) copy-start(f32[1,16,64]{2,1,0:T(8,128)} %copy.674) | copy-start | bytes 12292
  168.4 19.4 %copy-start.19 = (f32[1,16,64]{2,1,0:T(8,128)S(1)}, f32[1,16,64]{2,1,0:T(8,128)}, u32[]{:S(2)}) copy-start(f32[1,16,64]{2,1,0:T(8,128)} %copy.675) | copy-start | bytes 12292
  168.5 19.2 %copy-start.24 = (f32[1,16,64]{2,1,0:T(8,128)S(1)}, f32[1,16,64]{2,1,0:T(8,128)}, u32[]{:S(2)}) copy-start(f32[1,16,64]{2,1,0:T(8,128)} %copy.670) | copy-start | bytes 12292
  168.5 19.2 %copy-start.23 = (f32[1,16,64]{2,1,0:T(8,128)S(1)}, f32[1,16,64]{2,1,0:T(8,128)}, u32[]{:S(2)}) copy-start(f32[1,16,64]{2,1,0:T(8,128)} %copy.671) | copy-start | bytes 12292
  168.5 19.2 %copy-start.22 = (f32[1,16,64]{2,1,0:T(8,128)S(1)}, f32[1,16,64]{2,1,0:T(8,128)}, u32[]{:S(2)}) copy-start(f32[1,16,64]{2,1,0:T(8,128)} %copy.672) | copy-start | bytes 12292
  168.6 19.1 %copy-start.27 = (f32[1,16,64]{2,1,0:T(8,128)S(1)}, f32[1,16,64]{2,1,0:T(8,128)}, u32[]{:S(2)}) copy-start(f32[1,16,64]{2,1,0:T(8,128)} %copy.667) | copy-start | bytes 12292
  168.6 19.1 %copy-start.25 = (f32[1,16,64]{2,1,0:T(8,128)S(1)}, f32[1,16,64]{2,1,0:T(8,128)}, u32[]{:S(2)}) copy-start(f32[1,16,64]{2,1,0:T(8,128)} %copy.668) | copy-start | bytes 12292
  168.6 19.1 %copy-start.26 = (f32[1,16,64]{2,1,0:T(8,128)S(1)}, f32[1,16,64]{2,1,0:T(8,128)}, u32[]{:S(2)}) copy-start(f32[1,16,64]{2,1,0:T(8,128)} %copy.669) | copy-start | bytes 12292
  168.7 18.9 %copy-start.30 = (f32[1,16,64]{2,1,0:T(8,128)S(1)}, f32[1,16,64]{2,1,0:T(8,128)}, u32[]{:S(2)}) copy-start(f32[1,16,64]{2,1,0:T(8,128)} %copy.664) | copy-start | bytes 12292
  168.7 18.9 %copy-start.29 = (f32[1,16,64]{2,1,0:T(8,128)S(1)}, f32[1,16,64]{2,1,0:T(8,128)}, u32[]{:S(2)}) copy-start(f32[1,16,64]{2,1,0:T(8,128)} %copy.665) | copy-start | bytes 12292
  168.7 18.9 %copy-start.28 = (f32[1,16,64]{2,1,0:T(8,128)S(1)}, f32[1,16,64]{2,1,0:T(8,128)}, u32[]{:S(2)}) copy-start(f32[1,16,64]{2,1,0:T(8,128)} %copy.666) | copy-start | bytes 12292
  168.7 18.8 %copy-start.33 = (f32[1,16,64]{2,1,0:T(8,128)S(1)}, f32[1,16,64]{2,1,0:T(8,128)}, u32[]{:S(2)}) copy-start(f32[1,16,64]{2,1,0:T(8,128)} %copy.661) | copy-start | bytes 12292
  168.7 18.8 %copy-start.32 = (f32[1,16,64]{2,1,0:T(8,128)S(1)}, f32[1,16,64]{2,1,0:T(8,128)}, u32[]{:S(2)}) copy-start(f32[1,16,64]{2,1,0:T(8,128)} %copy.662) | copy-start | bytes 12292
  168.7 18.8 %copy-start.31 = (f32[1,16,64]{2,1,0:T(8,128)S(1)}, f32[1,16,64]{2,1,0:T(8,128)}, u32[]{:S(2)}) copy-start(f32[1,16,64]{2,1,0:T(8,128)} %copy.663) | copy-start | bytes 12292
  190.1 26.3 %all-to-all-start.2 = ((f32[128,1,1024]{2,1,0:T(1,128)}), f32[128,1,1024]{2,1,0:T(1,128)S(1)}, u32[]{:S(2)}, u32[]{:S(2)}) async-start(f32[128,1,1024]{2,1,0:T(1,128)} %reshape.544), calls=%async_computation.2 | async-start | bytes 1048576 | tf_op jit(solution)/shard_map/all_to_all | solution.py:112
  255.1 33.0 %copy-start.56 = (f32[2]{0:T(128)}, f32[2]{0:T(128)S(1)}, u32[]{:S(2)}) copy-start(f32[2]{0:T(128)S(1)} %div.6) | copy-start | bytes 28
  255.3 32.8 %copy-start.5 = (f32[2,16,2048]{2,1,0:T(8,128)}, f32[2,16,2048]{2,1,0:T(8,128)S(1)}, u32[]{:S(2)}) copy-start(f32[2,16,2048]{2,1,0:T(8,128)S(1)} %get-tuple-element.10) | copy-start | bytes 786436
  (36 other events, 427.2 us)
